TPU v7x, 256 devices: a whole 4x4x8 slice. The times are simulated.
256 devices in a mesh: tm: 64 (over y, z, core), space: 4 (over x).
Axes of the slice: x: 4, y: 4, z: 8, core: 2. Of those that a mesh axis runs over, the one named last changes fastest.
Arguments:
- residual: float32 [64, 2, 1024, 1024], P('tm', None, 'space'), may hold values from -0.875 to 0.875
- counts: int32 [64], P('tm'), may hold values from 1 to 4
Outputs:
- fields: float32 [64, 2, 1024, 1024], P('tm', None, 'space')
All inputs are finite; a program needn't handle non-finite values.
Results may differ from a plain program's by a relative error of at most 0.0003.
Values sent between devices are 32-bit elements; how exact they have to be, the bound alone decides.
A program may use at most 320 MiB of HBM per device.

v0:
```python
import functools
import math

import jax
import jax.numpy as jnp
import numpy as np
from jax import lax
from jax.experimental import pallas as pl
from jax.experimental.pallas import tpu as pltpu
from jax.sharding import Mesh
from jax.sharding import PartitionSpec as P

phase_rate = 0.004
F32 = jnp.float32
BF16 = jnp.bfloat16
MESH = pl.DeviceIdType.MESH
LANES = 128
FOLD = 64

SIN_TERMS = [(-1) ** i * math.pi ** (2 * i + 1) / math.factorial(2 * i + 1) for i in range(7)]
COS_TERMS = [(-1) ** i * math.pi ** (2 * i) / math.factorial(2 * i) for i in range(7)]


def cas_tables(length):
    half, quarter = length // 2, length // 4
    place = np.arange(length)
    wave = 2 * (place % half) + place // half
    phases = (np.arange(half)[:, None] * wave[None, :] % length) * (2.0 * math.pi / length)
    table = np.cos(phases) + np.sin(phases)
    table = table.reshape(half, 2, 2, quarter).transpose(1, 2, 0, 3)
    high = table.astype(BF16)
    low = (table - high.astype(np.float64)).astype(BF16)
    return high, low


def halves(x):
    high = x.astype(BF16)
    return high, (x - high.astype(F32)).astype(BF16)


def dot3(a_high, a_low, b_high, b_low):
    dot = functools.partial(jnp.dot, preferred_element_type=F32)
    return dot(a_high, b_high) + (dot(a_low, b_high) + dot(a_high, b_low))


def signed(wave, length):
    return jnp.where(wave < length // 2, wave, wave - length).astype(F32)


def kernel(
    sizes,
    count_ref, source, table_high, table_low, result,
    r, th, tl, xh, xl, sdh, sdl, sa, rb, bh, bl, f0, fs, cosines, sines, zb, tt, ty, ps, pb,
    qh, ql, xs, yb, lh, ll, eo, ob, c_own, c_mate, c_pair, c_z, c_row, c_y,
    load_sem, a_send, a_recv, z_send, z_recv, y_send, y_recv, p_send, p_recv, b_send, b_recv,
    cm_send, cm_recv, cz_send, cz_recv, cy_send, cy_recv, out_sem,
):
    Y, Z, X, N = sizes
    m, H, W, B, XH = N // X, N // 2, N // 4, N // Z, X // 2
    nb = W // B
    yi, zi, ci, xi = (lax.axis_index(a) for a in ("y", "z", "c", "x"))
    mate = 1 - ci
    low_lanes = lax.broadcasted_iota(jnp.int32, (1, LANES), 1) < FOLD

    def swap(x):
        return pltpu.roll(x, FOLD, axis=1)

    def remote(src, dst, send, recv, **where):
        return pltpu.make_async_remote_copy(
            src_ref=src, dst_ref=dst, send_sem=send, recv_sem=recv, device_id=where, device_id_type=MESH
        )

    def x_peers():
        return [(lax.rem(xi + o, X), lax.rem(ci + d, 2)) for o in range(X) for d in range(2) if o or d]

    def z_peers():
        order = sorted(range(1, Z), key=lambda o: -min(o, Z - o))
        return [lax.rem(zi + o, Z) for o in order]

    def chunks(total, rows, body):
        def step(i, carry):
            body(pl.multiple_of(i * rows, rows))
            return carry
        lax.fori_loop(0, total // rows, step, 0)

    def repeat(count, body):
        def step(i, carry):
            body(i)
            return carry
        lax.fori_loop(0, count, step, 0)

    loads = [
        pltpu.make_async_copy(source, r, load_sem.at[0]),
        pltpu.make_async_copy(table_high, th, load_sem.at[1]),
        pltpu.make_async_copy(table_low, tl, load_sem.at[2]),
    ]
    for load in loads:
        load.start()
    c_own[...] = jnp.full(c_own.shape, count_ref[0].astype(F32), F32)

    barrier = pltpu.get_barrier_semaphore()
    for x_to, c_to in x_peers():
        pl.semaphore_signal(barrier, inc=1, device_id={"x": x_to, "c": c_to}, device_id_type=MESH)
    for z_to in z_peers():
        pl.semaphore_signal(barrier, inc=1, device_id={"z": z_to}, device_id_type=MESH)
    for o in range(1, Y):
        pl.semaphore_signal(barrier, inc=1, device_id={"y": lax.rem(yi + o, Y)}, device_id_type=MESH)
    pl.semaphore_wait(barrier, 2 * X - 1 + Z - 1 + Y - 1)

    def to_mate():
        return remote(c_own, c_mate, cm_send, cm_recv, c=mate)

    def pair_to(o):
        return remote(c_pair, c_z.at[o], cz_send.at[o], cz_recv.at[o], z=lax.rem(zi + o, Z))

    def row_to(o):
        return remote(c_row, c_y.at[o], cy_send.at[o], cy_recv.at[o], y=lax.rem(yi + o, Y))

    to_mate().start()

    loads[0].wait()
    for comp in range(2):
        def split_rows(at, comp=comp):
            rows = pl.ds(at, 32)
            first, second = r[comp, rows, :H], r[comp, rows, H:]
            sdh[0, comp, rows, :], sdl[0, comp, rows, :] = halves(first + second)
            sdh[1, comp, rows, :], sdl[1, comp, rows, :] = halves(first - second)
        chunks(m, 32, split_rows)

    to_mate().wait_recv()
    c_pair[...] = c_own[...] + c_mate[...]
    for o in range(1, Z):
        pair_to(o).start()
    loads[1].wait()
    loads[2].wait()

    def a_copy(h, x_to, c_to):
        return remote(sa.at[h, x_to, c_to], rb.at[h, ci, xi], a_send.at[h, x_to, c_to], a_recv.at[h, xi, ci], x=x_to, c=c_to)

    def a_arrival(h, x_from, c_from):
        return remote(sa.at[h, x_from, c_from], rb.at[h, c_from, x_from], a_send.at[h, x_from, c_from],
                      a_recv.at[h, x_from, c_from], x=x_from, c=c_from)

    def along_y(i):
        h, par = i // 2, lax.rem(xi // XH + 1 + i, 2)
        w_part = dot3(sdh[par, 0], sdl[par, 0], th[par, h], tl[par, h])
        v_part = dot3(sdh[par, 1], sdl[par, 1], th[par, h], tl[par, h])
        for k in range(XH):
            x_to = par * XH + k
            wt, vt = w_part[:, k * LANES:(k + 1) * LANES], v_part[:, k * LANES:(k + 1) * LANES]
            sa[h, x_to, 0] = jnp.where(low_lanes, wt, swap(vt))
            sa[h, x_to, 1] = jnp.where(low_lanes, swap(wt), vt)
        for k in range(XH):
            x_to = par * XH + k

            @pl.when(x_to != xi)
            def _():
                a_copy(h, x_to, mate).start()
                a_copy(h, x_to, ci).start()

            @pl.when(x_to == xi)
            def _():
                a_copy(h, x_to, mate).start()
                rb[h, ci, xi] = sa[h, x_to, ci]

    repeat(2, along_y)

    base = jnp.zeros_like(c_own)
    row = c_pair[...]
    for o in range(1, Z):
        pair_to(o).wait_recv()
        row = row + c_z[o]
        base = base + jnp.where(zi >= o, c_z[o], 0.0)
    c_row[...] = row
    for o in range(1, Y):
        row_to(o).start()

    repeat(2, lambda i: along_y(i + 2))

    for par in range(2):
        for h in range(2):
            for k in range(2):
                xh[par, h, k] = th[par, h, k * W:(k + 1) * W, :].astype(F32).T.astype(BF16)
                xl[par, h, k] = tl[par, h, k * W:(k + 1) * W, :].astype(F32).T.astype(BF16)

    for o in range(1, Y):
        row_to(o).wait_recv()
        base = base + jnp.where(yi >= o, c_y[o], 0.0)
    first_count = jnp.where(ci == 0, c_own[...], c_mate[...])
    rates = [
        (base + first_count)[:1] * (phase_rate / math.pi),
        (base + c_pair[...])[:1] * (phase_rate / math.pi),
    ]
    terms = [jnp.where(low_lanes, s, c) for s, c in zip(SIN_TERMS, COS_TERMS)]
    lane = lax.rem(lax.broadcasted_iota(jnp.int32, (1, LANES), 1), FOLD)

    def angles(h):
        col = h * W + lax.rem(xi, XH) * LANES + ci * FOLD + lane
        wave_y = signed(2 * col + xi // XH, N)

        def rows_of(at):
            place = at + lax.broadcasted_iota(jnp.int32, (64, LANES), 0)
            wave_x = signed(2 * lax.rem(place, H) + place // H, N)
            modulus = jnp.sqrt(wave_x * wave_x + wave_y * wave_y)
            for t in range(2):
                turns = modulus * rates[t]
                nearest = jnp.floor(turns + 0.5)
                f = turns - nearest
                g = f * f
                value = terms[-1]
                for term in terms[-2::-1]:
                    value = value * g + term
                value = jnp.where(low_lanes, value * f, value)
                half = nearest * 0.5
                value = jnp.where(half == jnp.floor(half), value, -value)
                other = swap(value)
                cosines[h, t, pl.ds(at, 64), :] = jnp.where(low_lanes, other, value)
                sines[h, t, pl.ds(at, 64), :] = jnp.where(low_lanes, -value, other)
        chunks(N, 64, rows_of)

    repeat(2, angles)

    def z_copy(h, z_to):
        return remote(fs.at[h, pl.ds(pl.multiple_of(z_to * B, B), B)], zb.at[h, zi], z_send.at[h, z_to], z_recv.at[h, zi], z=z_to)

    def z_arrival(h, z_from):
        return remote(zb.at[h, z_from], zb.at[h, z_from], z_send.at[h, z_from], z_recv.at[h, z_from], z=z_from)

    def along_x(h):
        for x_from, c_from in x_peers():
            a_arrival(h, x_from, c_from).wait_recv()
        for k in range(XH):
            for t in range(2):
                def split_rows(at, k=k, t=t):
                    first, second = rb[h, t, k, pl.ds(at, 64), :], rb[h, t, k + XH, pl.ds(at, 64), :]
                    rows = pl.ds(pl.multiple_of(k * m + at, 64), 64)
                    lanes = slice(t * LANES, (t + 1) * LANES)
                    bh[0, rows, lanes], bl[0, rows, lanes] = halves(first + second)
                    bh[1, rows, lanes], bl[1, rows, lanes] = halves(first - second)
                chunks(m, 64, split_rows)

        def quarter(i):
            g = lax.rem(zi // nb + 2 + i, 4)
            par, q = g // 2, lax.rem(g, 2)
            high = jnp.concatenate([xh[par, q, 0], xh[par, q, 1]], axis=1)
            low = jnp.concatenate([xl[par, q, 0], xl[par, q, 1]], axis=1)
            found = dot3(high, low, bh[par], bl[par])
            rows = pl.ds(pl.multiple_of(g * W, W), W)
            z0, z1 = found[:, :LANES], found[:, LANES:]
            framed0 = cosines[h, 0, rows] * z0 + sines[h, 0, rows] * swap(z0)
            framed1 = cosines[h, 1, rows] * z1 + sines[h, 1, rows] * swap(z1)
            f0[h, rows] = framed0
            fs[h, rows] = framed0 + framed1
            for k in range(nb):
                z_to = g * nb + k

                @pl.when(z_to != zi)
                def _():
                    z_copy(h, z_to).start()

                @pl.when(z_to == zi)
                def _():
                    zb[h, zi] = fs[h, pl.ds(pl.multiple_of(z_to * B, B), B)]

        repeat(4, quarter)

    repeat(2, along_x)

    def y_copy(h, o):
        return remote(tt.at[h], ty.at[h, o], y_send.at[h, o], y_recv.at[h, o], y=lax.rem(yi + o, Y))

    def p_copy(h, z_to):
        return remote(ps.at[h, z_to], pb.at[h, zi], p_send.at[h, z_to], p_recv.at[h, zi], z=z_to)

    def p_arrival(h, z_from):
        return remote(ps.at[h, z_from], pb.at[h, z_from], p_send.at[h, z_from], p_recv.at[h, z_from], z=z_from)

    def prefix(h):
        for z_from in z_peers():
            z_arrival(h, z_from).wait_recv()
        total = zb[h, 0]
        for k in range(1, Z):
            total = total + zb[h, k]
        tt[h] = total
        for o in range(1, Y):
            y_copy(h, o).start()
        for o in range(1, Y):
            y_copy(h, o).wait_recv()
        running = jnp.zeros((B, LANES), F32)
        for o in range(1, Y):
            running = running + jnp.where(yi >= o, ty[h, o], 0.0)
        for k in range(Z):
            ps[h, k] = running
            running = running + zb[h, k]
        for z_to in z_peers():
            p_copy(h, z_to).start()
        pb[h, zi] = ps[h, zi]

    repeat(2, prefix)

    def b_copy(h, x_to, t):
        return remote(xs.at[h, x_to, t], yb.at[h, xi, ci], b_send.at[h, x_to, t], b_recv.at[h, xi, ci], x=x_to, c=t)

    def b_arrival(h, x_from, c_from):
        return remote(xs.at[h, x_from, c_from], yb.at[h, x_from, c_from], b_send.at[h, x_from, c_from],
                      b_recv.at[h, x_from, c_from], x=x_from, c=c_from)

    def back_x(h):
        for z_from in z_peers():
            p_arrival(h, z_from).wait_recv()

        def band(k):
            def rows_of(at):
                rows = pl.ds(pl.multiple_of(k * B + at, 64), 64)
                before = pb[h, k, pl.ds(at, 64), :]
                for t, own in ((0, f0), (1, fs)):
                    state = before + own[h, rows, :]
                    state = cosines[h, t, rows, :] * state - sines[h, t, rows, :] * swap(state)
                    lanes = slice(t * LANES, (t + 1) * LANES)
                    qh[rows, lanes], ql[rows, lanes] = halves(state * (1.0 / (N * N)))
            chunks(B, 64, rows_of)

        repeat(Z, band)

        def block(i):
            k = lax.rem(xi + 1 + i, XH)
            rows = pl.ds(pl.multiple_of(k * m, m), m)
            parts = []
            for par in range(2):
                high = jnp.concatenate([th[par, 0, rows], th[par, 1, rows]], axis=1)
                low = jnp.concatenate([tl[par, 0, rows], tl[par, 1, rows]], axis=1)
                waves = slice(par * H, (par + 1) * H)
                parts.append(dot3(high, low, qh[waves, :], ql[waves, :]))
            outs = (parts[0] + parts[1], parts[0] - parts[1])
            for j in range(2):
                for t in range(2):
                    xs[h, k + j * XH, t] = outs[j][:, t * LANES:(t + 1) * LANES]
            for j in range(2):
                x_to = k + j * XH

                @pl.when(x_to != xi)
                def _():
                    b_copy(h, x_to, mate).start()
                    b_copy(h, x_to, ci).start()

                @pl.when(x_to == xi)
                def _():
                    b_copy(h, x_to, mate).start()
                    yb[h, xi, ci] = xs[h, x_to, ci]

        repeat(XH, block)

    repeat(2, back_x)

    def back_y(h, last):
        for x_from, c_from in x_peers():
            b_arrival(h, x_from, c_from).wait_recv()
        for par in range(2):
            for k in range(XH):
                def split_rows(at, par=par, k=k):
                    rows = pl.ds(at, 64)
                    one, two = yb[h, par * XH + k, 0, rows, :], yb[h, par * XH + k, 1, rows, :]
                    lanes = slice(k * LANES, (k + 1) * LANES)
                    lh[par, 0, rows, lanes], ll[par, 0, rows, lanes] = halves(jnp.where(low_lanes, one, swap(two)))
                    lh[par, 1, rows, lanes], ll[par, 1, rows, lanes] = halves(jnp.where(low_lanes, swap(one), two))
                chunks(m, 64, split_rows)

        def component(comp):
            for k in range(2):
                parts = [dot3(lh[par, comp], ll[par, comp], xh[par, h, k], xl[par, h, k]) for par in range(2)]
                if last:
                    even, odd = (eo[comp, k, par] + parts[par] for par in range(2))
                    ob[comp, :, k * W:(k + 1) * W] = even + odd
                    ob[comp, :, H + k * W:H + (k + 1) * W] = even - odd
                else:
                    for par in range(2):
                        eo[comp, k, par] = parts[par]
            if last:
                pltpu.make_async_copy(ob.at[comp], result.at[comp], out_sem.at[comp]).start()

        repeat(2, component)

    back_y(0, False)
    back_y(1, True)

    for comp in range(2):
        pltpu.make_async_copy(ob.at[comp], result.at[comp], out_sem.at[comp]).wait()
    to_mate().wait_send()
    for o in range(1, Z):
        pair_to(o).wait_send()
    for o in range(1, Y):
        row_to(o).wait_send()

    def sent(h):
        for x_to, c_to in x_peers():
            a_copy(h, x_to, c_to).wait_send()
            b_copy(h, x_to, c_to).wait_send()
        for z_to in z_peers():
            z_copy(h, z_to).wait_send()
            p_copy(h, z_to).wait_send()
        for o in range(1, Y):
            y_copy(h, o).wait_send()

    repeat(2, sent)


def call(sizes, residual, counts, high, low):
    Y, Z, X, N = sizes
    m, H, W, B = N // X, N // 2, N // 4, N // Z
    vmem, dma = pltpu.VMEM, pltpu.SemaphoreType.DMA
    anywhere = pl.BlockSpec(memory_space=pl.ANY)
    tile = vmem((8, LANES), F32)
    return pl.pallas_call(
        functools.partial(kernel, sizes),
        out_shape=jax.ShapeDtypeStruct((2, m, N), F32),
        in_specs=[pl.BlockSpec(memory_space=pltpu.SMEM), anywhere, anywhere, anywhere],
        out_specs=anywhere,
        scratch_shapes=[
            vmem((2, m, N), F32),
            vmem((2, 2, H, W), BF16), vmem((2, 2, H, W), BF16),
            vmem((2, 2, 2, W, W), BF16), vmem((2, 2, 2, W, W), BF16),
            vmem((2, 2, m, H), BF16), vmem((2, 2, m, H), BF16),
            vmem((2, X, 2, m, LANES), F32),
            vmem((2, 2, X, m, LANES), F32),
            vmem((2, H, 2 * LANES), BF16), vmem((2, H, 2 * LANES), BF16),
            vmem((2, N, LANES), F32), vmem((2, N, LANES), F32),
            vmem((2, 2, N, LANES), F32), vmem((2, 2, N, LANES), F32),
            vmem((2, Z, B, LANES), F32),
            vmem((2, B, LANES), F32), vmem((2, Y, B, LANES), F32),
            vmem((2, Z, B, LANES), F32), vmem((2, Z, B, LANES), F32),
            vmem((N, 2 * LANES), BF16), vmem((N, 2 * LANES), BF16),
            vmem((2, X, 2, m, LANES), F32), vmem((2, X, 2, m, LANES), F32),
            vmem((2, 2, m, W), BF16), vmem((2, 2, m, W), BF16),
            vmem((2, 2, 2, m, W), F32),
            vmem((2, m, N), F32),
            tile, tile, tile, vmem((Z, 8, LANES), F32), tile, vmem((Y, 8, LANES), F32),
            dma((3,)),
            dma((2, X, 2)), dma((2, X, 2)),
            dma((2, Z)), dma((2, Z)),
            dma((2, Y)), dma((2, Y)),
            dma((2, Z)), dma((2, Z)),
            dma((2, X, 2)), dma((2, X, 2)),
            dma, dma, dma((Z,)), dma((Z,)), dma((Y,)), dma((Y,)),
            dma((2,)),
        ],
        compiler_params=pltpu.CompilerParams(
            collective_id=0, has_side_effects=True, vmem_limit_bytes=60 * 1024 * 1024
        ),
        name="wave",
    )(counts, residual, high, low)


def built(split, length):
    sizes = tuple(split.shape[a] for a in ("y", "z", "x")) + (length,)
    high, low = cas_tables(length)

    def on_device(residual, counts):
        return call(sizes, residual[0], counts, jnp.asarray(high), jnp.asarray(low))[None]

    times = ("y", "z", "c")
    return jax.shard_map(
        on_device,
        mesh=split,
        in_specs=(P(times, None, "x", None), P(times)),
        out_specs=P(times, None, "x", None),
        check_vma=False,
    )


def solution(mesh):
    points, spaces = mesh.shape["tm"], mesh.shape["space"]
    split = Mesh(mesh.devices.reshape(4, points // 8, 2, spaces), ("y", "z", "c", "x"))
    return built(split, 1024)
```

profile of v0, /device:TPU:1, one launch (start us, length us, event | category | flops | bytes accessed | tf_op | source)
XLA Modules:
  0.0 97.5 jit_solution(12066965777554896375)
XLA Ops:
  0.7 93.7 %wave.1 = f32[2,256,1024]{2,1,0:T(8,128)} custom-call(s32[1]{0:T(128)S(6)} %copy.6.count_ref, f32[2,256,1024]{2,1,0:T(8,128)} %bitcast.3, bf16[2,2,512,256]{3,2,1,0:T(8,128)(2,1)} %constant.4.clone.table_high, bf16[2,2,512,256]{3,2,1,0:T(8,128)(2,1)} %constant.5.clone.table_low), custom_call_target="tpu_custom_call" | custom-call | tf_op jit(solution)/shard_map/wave/pallas_call | solution.py:413
  94.3 3.2 %copy.7 = f32[1,2,256,1024]{3,2,1,0:T(8,128)} copy(f32[1,2,256,1024]{3,2,1,0:T(8,128)} %bitcast.2) | data formatting | bytes 4194304
where the time goes:
time: 97.6 us; the launch traced here: 97.5 us
  Pallas kernels  93.7 us (96%)
  local copies, waits for them, and re-layouts  3.16 us (3%)
    pallas_call x1, Pallas kernels, call(): pl.pallas_call(functools.partial(kernel, sizes), out_shape=jax.ShapeDtype...  93.7 us
    unnamed x1, local copies, waits for them, and re-layouts  3.16 us

commit v1 on v0

v1 whole, which is shorter than its diff:
```python
import functools
import math

import jax
import jax.numpy as jnp
import numpy as np
from jax import lax
from jax.experimental import pallas as pl
from jax.experimental.pallas import tpu as pltpu
from jax.sharding import Mesh
from jax.sharding import PartitionSpec as P

phase_rate = 0.004
F32 = jnp.float32
BF16 = jnp.bfloat16
MESH = pl.DeviceIdType.MESH
LANES = 128
FOLD = 32
CHUNKS = 4

SIN_TERMS = [(-1) ** i * math.pi ** (2 * i + 1) / math.factorial(2 * i + 1) for i in range(7)]
COS_TERMS = [(-1) ** i * math.pi ** (2 * i) / math.factorial(2 * i) for i in range(7)]


def cas_tables(length):
    half, quarter = length // 2, length // 4
    place = np.arange(length)
    wave = 2 * (place % half) + place // half
    phases = (np.arange(half)[:, None] * wave[None, :] % length) * (2.0 * math.pi / length)
    table = np.cos(phases) + np.sin(phases)
    table = table.reshape(half, 2, 2, quarter).transpose(1, 2, 0, 3)
    high = table.astype(BF16)
    low = (table - high.astype(np.float64)).astype(BF16)
    return high, low


def halves(x):
    high = x.astype(BF16)
    return high, (x - high.astype(F32)).astype(BF16)


def dot3(a_high, a_low, b_high, b_low):
    dot = functools.partial(jnp.dot, preferred_element_type=F32)
    return dot(a_high, b_high) + (dot(a_low, b_high) + dot(a_high, b_low))


def product(high, low, packed):
    dot = functools.partial(jnp.dot, preferred_element_type=F32)
    both = dot(high, packed)
    return both[:, :LANES] + (both[:, LANES:] + dot(low, packed[:, :LANES]))


def signed(wave, length):
    return jnp.where(wave < length // 2, wave, wave - length).astype(F32)


def kernel(
    sizes,
    count_ref, source, table_high, table_low, result,
    r, th, tl, xh, xl, sdh, sdl, sa, rb, mix, own, fs, cosines, sines, zb, tt, ty, ps, pb,
    q, xs, yb, lh, ll, eo, ob, c_own, c_mate, c_pair, c_z, c_row, c_y,
    load_sem, a_send, a_recv, z_send, z_recv, y_send, y_recv, p_send, p_recv, b_send, b_recv,
    cm_send, cm_recv, cz_send, cz_recv, cy_send, cy_recv, out_sem,
):
    Y, Z, X, N = sizes
    m, H, W, B, XH = N // X, N // 2, N // 4, N // Z, X // 2
    nb, m2, B2 = W // B, m // 2, B // 2
    yi, zi, ci, xi = (lax.axis_index(a) for a in ("y", "z", "c", "x"))
    mate = 1 - ci
    lane = lax.broadcasted_iota(jnp.int32, (1, LANES), 1)
    first_half = lane < 2 * FOLD
    w_lanes = lax.rem(lane, 2 * FOLD) < FOLD

    def turn(x, lanes):
        return pltpu.roll(x, lanes, axis=1)

    def swap(x):
        return jnp.where(w_lanes, turn(x, LANES - FOLD), turn(x, FOLD))

    def cross(a, b):
        return jnp.where(first_half, a, turn(b, 2 * FOLD)), jnp.where(first_half, turn(a, 2 * FOLD), b)

    def weave(a, b):
        return jnp.where(w_lanes, a, turn(b, FOLD)), jnp.where(w_lanes, turn(a, LANES - FOLD), b)

    def remote(src, dst, send, recv, **where):
        return pltpu.make_async_remote_copy(
            src_ref=src, dst_ref=dst, send_sem=send, recv_sem=recv, device_id=where, device_id_type=MESH
        )

    def x_peers():
        return [(lax.rem(xi + o, X), lax.rem(ci + d, 2)) for o in range(X) for d in range(2) if o or d]

    def z_peers():
        order = sorted(range(1, Z), key=lambda o: -min(o, Z - o))
        return [lax.rem(zi + o, Z) for o in order]

    def chunks(total, rows, body):
        def step(i, carry):
            body(pl.multiple_of(i * rows, rows))
            return carry
        lax.fori_loop(0, total // rows, step, 0)

    def repeat(count, body):
        def step(i, carry):
            body(i)
            return carry
        lax.fori_loop(0, count, step, 0)

    loads = [
        pltpu.make_async_copy(source, r, load_sem.at[0]),
        pltpu.make_async_copy(table_high, th, load_sem.at[1]),
        pltpu.make_async_copy(table_low, tl, load_sem.at[2]),
    ]
    for load in loads:
        load.start()
    c_own[...] = jnp.full(c_own.shape, count_ref[0].astype(F32), F32)

    barrier = pltpu.get_barrier_semaphore()
    for x_to, c_to in x_peers():
        pl.semaphore_signal(barrier, inc=1, device_id={"x": x_to, "c": c_to}, device_id_type=MESH)
    for z_to in z_peers():
        pl.semaphore_signal(barrier, inc=1, device_id={"z": z_to}, device_id_type=MESH)
    for o in range(1, Y):
        pl.semaphore_signal(barrier, inc=1, device_id={"y": lax.rem(yi + o, Y)}, device_id_type=MESH)
    pl.semaphore_wait(barrier, 2 * X - 1 + Z - 1 + Y - 1)

    def to_mate():
        return remote(c_own, c_mate, cm_send, cm_recv, c=mate)

    def pair_to(o):
        return remote(c_pair, c_z.at[o], cz_send.at[o], cz_recv.at[o], z=lax.rem(zi + o, Z))

    def row_to(o):
        return remote(c_row, c_y.at[o], cy_send.at[o], cy_recv.at[o], y=lax.rem(yi + o, Y))

    to_mate().start()

    loads[0].wait()
    for comp in range(2):
        def split_rows(at, comp=comp):
            rows = pl.ds(at, 32)
            first, second = r[comp, rows, :H], r[comp, rows, H:]
            sdh[0, comp, rows, :], sdl[0, comp, rows, :] = halves(first + second)
            sdh[1, comp, rows, :], sdl[1, comp, rows, :] = halves(first - second)
        chunks(m, 32, split_rows)

    loads[1].wait()
    loads[2].wait()

    def a_copy(h, x_to, c_to):
        return remote(sa.at[h, x_to, c_to], rb.at[h, ci, xi], a_send.at[h, x_to, c_to], a_recv.at[h, xi, ci], x=x_to, c=c_to)

    def a_arrival(h, x_from, c_from):
        return remote(sa.at[h, x_from, c_from], rb.at[h, c_from, x_from], a_send.at[h, x_from, c_from],
                      a_recv.at[h, x_from, c_from], x=x_from, c=c_from)

    def along_y(i):
        pair, par = i // 2, lax.rem(xi // XH + 1 + i, 2)
        w_part = dot3(sdh[par, 0], sdl[par, 0], th[par, pair], tl[par, pair])
        v_part = dot3(sdh[par, 1], sdl[par, 1], th[par, pair], tl[par, pair])
        for j in range(2):
            lanes = slice(j * LANES, (j + 1) * LANES)
            w_tiles = cross(w_part[:m2, lanes], w_part[m2:, lanes])
            v_tiles = cross(v_part[:m2, lanes], v_part[m2:, lanes])
            for k in range(XH):
                sa[2 * pair + j, par * XH + k, 0], sa[2 * pair + j, par * XH + k, 1] = weave(w_tiles[k], v_tiles[k])

    def send_along_y(h, q):
        par = lax.rem(xi // XH + 1 + q, 2)
        for k in range(XH):
            x_to = par * XH + k

            @pl.when(x_to != xi)
            def _():
                a_copy(h, x_to, mate).start()
                a_copy(h, x_to, ci).start()

            @pl.when(x_to == xi)
            def _():
                a_copy(h, x_to, mate).start()
                rb[h, ci, xi] = sa[h, x_to, ci]

    def first_stage(pair):
        along_y(2 * pair)
        send_along_y(2 * pair, 0)
        along_y(2 * pair + 1)
        send_along_y(2 * pair, 1)
        send_along_y(2 * pair + 1, 0)
        send_along_y(2 * pair + 1, 1)

    first_stage(0)
    to_mate().wait_recv()
    c_pair[...] = c_own[...] + c_mate[...]
    for o in range(1, Z):
        pair_to(o).start()
    first_stage(1)

    base = jnp.zeros_like(c_own)
    row = c_pair[...]
    for o in range(1, Z):
        pair_to(o).wait_recv()
        row = row + c_z[o]
        base = base + jnp.where(zi >= o, c_z[o], 0.0)
    c_row[...] = row
    for o in range(1, Y):
        row_to(o).start()

    for par in range(2):
        for h in range(2):
            for k in range(2):
                xh[par, h, k] = th[par, h, k * W:(k + 1) * W, :].astype(F32).T.astype(BF16)
                xl[par, h, k] = tl[par, h, k * W:(k + 1) * W, :].astype(F32).T.astype(BF16)

    for o in range(1, Y):
        row_to(o).wait_recv()
        base = base + jnp.where(yi >= o, c_y[o], 0.0)
    first_count = jnp.where(ci == 0, c_own[...], c_mate[...])
    rates = jnp.where(first_half, (base + first_count)[:1], (base + c_pair[...])[:1]) * (phase_rate / math.pi)
    terms = [jnp.where(w_lanes, s, c) for s, c in zip(SIN_TERMS, COS_TERMS)]
    column = lax.rem(lane, FOLD)

    def angles(h):
        col = h * LANES + lax.rem(xi, XH) * 2 * FOLD + ci * FOLD + column
        wave_y = signed(2 * col + xi // XH, N)

        def rows_of(at):
            place = at + lax.broadcasted_iota(jnp.int32, (64, LANES), 0)
            wave_x = signed(2 * lax.rem(place, H) + place // H, N)
            turns = jnp.sqrt(wave_x * wave_x + wave_y * wave_y) * rates
            nearest = jnp.floor(turns + 0.5)
            f = turns - nearest
            g = f * f
            value = terms[-1]
            for term in terms[-2::-1]:
                value = value * g + term
            value = jnp.where(w_lanes, value * f, value)
            half = nearest * 0.5
            value = jnp.where(half == jnp.floor(half), value, -value)
            other = swap(value)
            cosines[h, pl.ds(at, 64), :] = jnp.where(w_lanes, other, value)
            sines[h, pl.ds(at, 64), :] = jnp.where(w_lanes, -value, other)
        chunks(N, 64, rows_of)

    def z_copy(h, z_to):
        return remote(fs.at[h, z_to], zb.at[h, zi], z_send.at[h, z_to], z_recv.at[h, zi], z=z_to)

    def z_arrival(h, z_from):
        return remote(zb.at[h, z_from], zb.at[h, z_from], z_send.at[h, z_from], z_recv.at[h, z_from], z=z_from)

    def along_x(h):
        for x_from, c_from in x_peers():
            a_arrival(h, x_from, c_from).wait_recv()
        for k in range(XH):
            def split_rows(at, k=k):
                def place(par, half, x):
                    rows = pl.ds(pl.multiple_of(k * m + half * m2 + at, 64), 64)
                    mix[par, rows, :LANES], mix[par, rows, LANES:] = halves(x)
                near = [rb[h, t, k, pl.ds(at, 64), :] for t in range(2)]
                far = [rb[h, t, k + XH, pl.ds(at, 64), :] for t in range(2)]
                for half, x in enumerate(cross(near[0] + far[0], near[1] + far[1])):
                    place(0, half, x)
                for half, x in enumerate(cross(near[0] - far[0], near[1] - far[1])):
                    place(1, half, x)
            chunks(m2, 64, split_rows)

        def quarter(i):
            g = lax.rem(zi // nb + 2 + i, 4)
            par, half = g // 2, lax.rem(g, 2)
            high = jnp.concatenate([xh[par, half, 0], xh[par, half, 1]], axis=1)
            low = jnp.concatenate([xl[par, half, 0], xl[par, half, 1]], axis=1)
            found = product(high, low, mix[par])
            rows = pl.ds(pl.multiple_of(g * W, W), W)
            framed = cosines[h, rows] * found + sines[h, rows] * swap(found)
            framed = framed + jnp.where(first_half, 0.0, turn(framed, 2 * FOLD))
            own[h, rows] = framed
            for k in range(nb):
                z_to = g * nb + k
                a, b = framed[k * B:k * B + B2], framed[k * B + B2:(k + 1) * B]
                fs[h, z_to] = jnp.where(first_half, turn(a, 2 * FOLD), b)
            for k in range(nb):
                z_to = g * nb + k

                @pl.when(z_to != zi)
                def _():
                    z_copy(h, z_to).start()

                @pl.when(z_to == zi)
                def _():
                    zb[h, zi] = fs[h, zi]

        repeat(4, quarter)

    def y_copy(h, o):
        return remote(tt.at[h], ty.at[h, o], y_send.at[h, o], y_recv.at[h, o], y=lax.rem(yi + o, Y))

    def p_copy(h, z_to):
        return remote(ps.at[h, z_to], pb.at[h, zi], p_send.at[h, z_to], p_recv.at[h, zi], z=z_to)

    def p_arrival(h, z_from):
        return remote(ps.at[h, z_from], pb.at[h, z_from], p_send.at[h, z_from], p_recv.at[h, z_from], z=z_from)

    def totals(h):
        for z_from in z_peers():
            z_arrival(h, z_from).wait_recv()
        total = zb[h, 0]
        for k in range(1, Z):
            total = total + zb[h, k]
        tt[h] = total
        for o in range(1, Y):
            y_copy(h, o).start()

    def prefix(h):
        for o in range(1, Y):
            y_copy(h, o).wait_recv()
        running = jnp.zeros((B2, LANES), F32)
        for o in range(1, Y):
            running = running + jnp.where(yi >= o, ty[h, o], 0.0)
        for k in range(Z):
            ps[h, k] = running
            running = running + zb[h, k]
        for z_to in z_peers():
            p_copy(h, z_to).start()
        pb[h, zi] = ps[h, zi]

    def forward(i):
        angles(i)
        along_x(i)

    repeat(3, forward)
    totals(0)
    forward(3)

    def middle(i):
        totals(i + 1)
        prefix(i)

    repeat(3, middle)
    prefix(3)

    def b_copy(h, x_to, t):
        return remote(xs.at[h, x_to, t], yb.at[h, xi, ci], b_send.at[h, x_to, t], b_recv.at[h, xi, ci], x=x_to, c=t)

    def b_arrival(h, x_from, c_from):
        return remote(xs.at[h, x_from, c_from], yb.at[h, x_from, c_from], b_send.at[h, x_from, c_from],
                      b_recv.at[h, x_from, c_from], x=x_from, c=c_from)

    def back_x(h):
        for z_from in z_peers():
            p_arrival(h, z_from).wait_recv()

        def band(k):
            before = pb[h, k]
            for half, x in enumerate(cross(before, before)):
                rows = pl.ds(pl.multiple_of(k * B + half * B2, B2), B2)
                state = x + own[h, rows, :]
                state = cosines[h, rows, :] * state - sines[h, rows, :] * swap(state)
                q[rows, :LANES], q[rows, LANES:] = halves(state)

        repeat(Z, band)

        def block(i):
            k = lax.rem(xi + 1 + i, XH)
            rows = pl.ds(pl.multiple_of(k * m, m), m)
            parts = []
            for par in range(2):
                high = jnp.concatenate([th[par, 0, rows], th[par, 1, rows]], axis=1)
                low = jnp.concatenate([tl[par, 0, rows], tl[par, 1, rows]], axis=1)
                parts.append(product(high, low, q[par * H:(par + 1) * H]))
            for j, out in enumerate((parts[0] + parts[1], parts[0] - parts[1])):
                xs[h, k + j * XH, 0], xs[h, k + j * XH, 1] = cross(out[:m2], out[m2:])
            for j in range(2):
                x_to = k + j * XH

                @pl.when(x_to != xi)
                def _():
                    b_copy(h, x_to, mate).start()
                    b_copy(h, x_to, ci).start()

                @pl.when(x_to == xi)
                def _():
                    b_copy(h, x_to, mate).start()
                    yb[h, xi, ci] = xs[h, x_to, ci]

        repeat(XH, block)

    repeat(CHUNKS, back_x)

    def back_y(pair, last):
        for j in range(2):
            for x_from, c_from in x_peers():
                b_arrival(2 * pair + j, x_from, c_from).wait_recv()
        for par in range(2):
            for j in range(2):
                def split_rows(at, par=par, j=j):
                    tiles = [weave(yb[2 * pair + j, par * XH + k, 0, pl.ds(at, 64), :],
                                   yb[2 * pair + j, par * XH + k, 1, pl.ds(at, 64), :]) for k in range(XH)]
                    lanes = slice(j * LANES, (j + 1) * LANES)
                    for comp in range(2):
                        for half, x in enumerate(cross(tiles[0][comp], tiles[1][comp])):
                            rows = pl.ds(pl.multiple_of(half * m2 + at, 64), 64)
                            lh[par, comp, rows, lanes], ll[par, comp, rows, lanes] = halves(x)
                chunks(m2, 64, split_rows)

        def component(comp):
            for k in range(2):
                parts = [dot3(lh[par, comp], ll[par, comp], xh[par, pair, k], xl[par, pair, k]) for par in range(2)]
                if last:
                    even, odd = (eo[comp, k, par] + parts[par] for par in range(2))
                    ob[comp, :, k * W:(k + 1) * W] = even + odd
                    ob[comp, :, H + k * W:H + (k + 1) * W] = even - odd
                else:
                    for par in range(2):
                        eo[comp, k, par] = parts[par]
            if last:
                pltpu.make_async_copy(ob.at[comp], result.at[comp], out_sem.at[comp]).start()

        repeat(2, component)

    back_y(0, False)
    back_y(1, True)

    for comp in range(2):
        pltpu.make_async_copy(ob.at[comp], result.at[comp], out_sem.at[comp]).wait()
    to_mate().wait_send()
    for o in range(1, Z):
        pair_to(o).wait_send()
    for o in range(1, Y):
        row_to(o).wait_send()

    def sent(h):
        for x_to, c_to in x_peers():
            a_copy(h, x_to, c_to).wait_send()
            b_copy(h, x_to, c_to).wait_send()
        for z_to in z_peers():
            z_copy(h, z_to).wait_send()
            p_copy(h, z_to).wait_send()
        for o in range(1, Y):
            y_copy(h, o).wait_send()

    repeat(CHUNKS, sent)


def call(sizes, residual, counts, high, low):
    Y, Z, X, N = sizes
    m, H, W, B = N // X, N // 2, N // 4, N // Z
    vmem, dma = pltpu.VMEM, pltpu.SemaphoreType.DMA
    anywhere = pl.BlockSpec(memory_space=pl.ANY)
    tile = vmem((8, LANES), F32)
    return pl.pallas_call(
        functools.partial(kernel, sizes),
        out_shape=jax.ShapeDtypeStruct((2, m, N), F32),
        in_specs=[pl.BlockSpec(memory_space=pltpu.SMEM), anywhere, anywhere, anywhere],
        out_specs=anywhere,
        scratch_shapes=[
            vmem((2, m, N), F32),
            vmem((2, 2, H, W), BF16), vmem((2, 2, H, W), BF16),
            vmem((2, 2, 2, W, W), BF16), vmem((2, 2, 2, W, W), BF16),
            vmem((2, 2, m, H), BF16), vmem((2, 2, m, H), BF16),
            vmem((CHUNKS, X, 2, m // 2, LANES), F32),
            vmem((CHUNKS, 2, X, m // 2, LANES), F32),
            vmem((2, H, 2 * LANES), BF16),
            vmem((CHUNKS, N, LANES), F32),
            vmem((CHUNKS, Z, B // 2, LANES), F32),
            vmem((CHUNKS, N, LANES), F32), vmem((CHUNKS, N, LANES), F32),
            vmem((CHUNKS, Z, B // 2, LANES), F32),
            vmem((CHUNKS, B // 2, LANES), F32), vmem((CHUNKS, Y, B // 2, LANES), F32),
            vmem((CHUNKS, Z, B // 2, LANES), F32), vmem((CHUNKS, Z, B // 2, LANES), F32),
            vmem((N, 2 * LANES), BF16),
            vmem((CHUNKS, X, 2, m // 2, LANES), F32), vmem((CHUNKS, X, 2, m // 2, LANES), F32),
            vmem((2, 2, m, W), BF16), vmem((2, 2, m, W), BF16),
            vmem((2, 2, 2, m, W), F32),
            vmem((2, m, N), F32),
            tile, tile, tile, vmem((Z, 8, LANES), F32), tile, vmem((Y, 8, LANES), F32),
            dma((3,)),
            dma((CHUNKS, X, 2)), dma((CHUNKS, X, 2)),
            dma((CHUNKS, Z)), dma((CHUNKS, Z)),
            dma((CHUNKS, Y)), dma((CHUNKS, Y)),
            dma((CHUNKS, Z)), dma((CHUNKS, Z)),
            dma((CHUNKS, X, 2)), dma((CHUNKS, X, 2)),
            dma, dma, dma((Z,)), dma((Z,)), dma((Y,)), dma((Y,)),
            dma((2,)),
        ],
        compiler_params=pltpu.CompilerParams(
            collective_id=0, has_side_effects=True, vmem_limit_bytes=60 * 1024 * 1024
        ),
        name="wave",
    )(counts, residual, high, low)


def built(split, length):
    sizes = tuple(split.shape[a] for a in ("y", "z", "x")) + (length,)
    high, low = cas_tables(length)

    def on_device(residual, counts):
        return call(sizes, residual[0], counts, jnp.asarray(high), jnp.asarray(low))[None] * (1.0 / (length * length))

    times = ("y", "z", "c")
    return jax.shard_map(
        on_device,
        mesh=split,
        in_specs=(P(times, None, "x", None), P(times)),
        out_specs=P(times, None, "x", None),
        check_vma=False,
    )


def solution(mesh):
    points, spaces = mesh.shape["tm"], mesh.shape["space"]
    split = Mesh(mesh.devices.reshape(4, points // 8, 2, spaces), ("y", "z", "c", "x"))
    return built(split, 1024)
```

time: 97.6 us -> 90.8 us (0.930)
  Pallas kernels: 93.7 us -> 86.8 us
  other arithmetic: 0 us -> 3.22 us
  local copies, waits for them, and re-layouts: 3.16 us -> 0 us
    pallas_call x1, Pallas kernels: 93.7 us -> 86.8 us  [call(): pl.pallas_call(functools.partial(kernel, sizes), out_shape=jax.ShapeDtype...]
    mul x0 -> x1, other arithmetic: none -> 3.22 us  [on_device(): call(sizes, residual[0], counts, jnp.asarray(high), jnp.asarray(low))[None]]
    unnamed x1 -> x0, local copies, waits for them, and re-layouts: 3.16 us -> none
where the time goes in v1:
time: 90.8 us; the launch traced here: 90.7 us
  Pallas kernels  86.8 us (96%)
  other arithmetic  3.22 us (4%)
    pallas_call x1, Pallas kernels, call(): pl.pallas_call(functools.partial(kernel, sizes), out_shape=jax.ShapeDtype...  86.8 us
    mul x1, other arithmetic, on_device(): call(sizes, residual[0], counts, jnp.asarray(high), jnp.asarray(low))[None]  3.22 us

profile of v1, /device:TPU:1, one launch (start us, length us, event | category | flops | bytes accessed | tf_op | source)
XLA Modules:
  0.0 90.7 jit_solution(8674508085753223630)
XLA Ops:
  0.7 86.8 %wave.1 = f32[2,256,1024]{2,1,0:T(8,128)} custom-call(s32[1]{0:T(128)S(6)} %copy.5.count_ref, f32[2,256,1024]{2,1,0:T(8,128)} %bitcast.3, bf16[2,2,512,256]{3,2,1,0:T(8,128)(2,1)} %constant.6.clone.table_high, bf16[2,2,512,256]{3,2,1,0:T(8,128)(2,1)} %constant.7.clone.table_low), custom_call_target="tpu_custom_call" | custom-call | tf_op jit(solution)/shard_map/wave/pallas_call | solution.py:450
  87.5 3.2 %multiply_bitcast_fusion = f32[1,2,256,1024]{3,2,1,0:T(8,128)} fusion(f32[2,256,1024]{2,1,0:T(8,128)} %wave.1), kind=kLoop, calls=%fused_computation | loop fusion | flops 524288 | bytes 4194304 | tf_op jit(solution)/shard_map/mul | solution.py:496

commit v2 on v1

--- a/solution.py
+++ b/solution.py
@@ -58,9 +58,9 @@
     sizes,
     count_ref, source, table_high, table_low, result,
     r, th, tl, xh, xl, sdh, sdl, sa, rb, mix, own, fs, cosines, sines, zb, tt, ty, ps, pb,
-    q, xs, yb, lh, ll, eo, ob, c_own, c_mate, c_pair, c_z, c_row, c_y,
+    q, xs, yb, lh, ll, eo, c_own, c_mate, c_pair, c_z, c_row, c_y,
     load_sem, a_send, a_recv, z_send, z_recv, y_send, y_recv, p_send, p_recv, b_send, b_recv,
-    cm_send, cm_recv, cz_send, cz_recv, cy_send, cy_recv, out_sem,
+    cm_send, cm_recv, cz_send, cz_recv, cy_send, cy_recv, ready, go,
 ):
     Y, Z, X, N = sizes
     m, H, W, B, XH = N // X, N // 2, N // 4, N // Z, X // 2
@@ -114,16 +114,41 @@
     ]
     for load in loads:
         load.start()
-    c_own[...] = jnp.full(c_own.shape, count_ref[0].astype(F32), F32)
 
     barrier = pltpu.get_barrier_semaphore()
+    lead = jnp.logical_and(xi == 0, ci == 1)
     for x_to, c_to in x_peers():
-        pl.semaphore_signal(barrier, inc=1, device_id={"x": x_to, "c": c_to}, device_id_type=MESH)
-    for z_to in z_peers():
-        pl.semaphore_signal(barrier, inc=1, device_id={"z": z_to}, device_id_type=MESH)
-    for o in range(1, Y):
-        pl.semaphore_signal(barrier, inc=1, device_id={"y": lax.rem(yi + o, Y)}, device_id_type=MESH)
-    pl.semaphore_wait(barrier, 2 * X - 1 + Z - 1 + Y - 1)
+        @pl.when(jnp.logical_not(jnp.logical_and(x_to == 0, c_to == 1)))
+        def _():
+            pl.semaphore_signal(barrier, inc=1, device_id={"x": x_to, "c": c_to}, device_id_type=MESH)
+
+    def group_is_here():
+        @pl.when(jnp.logical_not(lead))
+        def _():
+            pl.semaphore_wait(barrier, 2 * X - 1)
+
+        @pl.when(jnp.logical_and(xi == 0, ci == 0))
+        def _():
+            pl.semaphore_signal(ready, inc=1, device_id={"c": mate}, device_id_type=MESH)
+
+        @pl.when(lead)
+        def _():
+            pl.semaphore_wait(ready, 1)
+            for z_to in z_peers():
+                pl.semaphore_signal(barrier, inc=1, device_id={"z": z_to}, device_id_type=MESH)
+            for o in range(1, Y):
+                pl.semaphore_signal(barrier, inc=1, device_id={"y": lax.rem(yi + o, Y)}, device_id_type=MESH)
+
+    def all_are_here():
+        @pl.when(lead)
+        def _():
+            pl.semaphore_wait(barrier, Z - 1 + Y - 1)
+            for x_to, c_to in x_peers():
+                pl.semaphore_signal(go, inc=1, device_id={"x": x_to, "c": c_to}, device_id_type=MESH)
+
+        @pl.when(jnp.logical_not(lead))
+        def _():
+            pl.semaphore_wait(go, 1)
 
     def to_mate():
         return remote(c_own, c_mate, cm_send, cm_recv, c=mate)
@@ -133,8 +158,6 @@
 
     def row_to(o):
         return remote(c_row, c_y.at[o], cy_send.at[o], cy_recv.at[o], y=lax.rem(yi + o, Y))
-
-    to_mate().start()
 
     loads[0].wait()
     for comp in range(2):
@@ -181,20 +204,24 @@
                 a_copy(h, x_to, mate).start()
                 rb[h, ci, xi] = sa[h, x_to, ci]
 
-    def first_stage(pair):
-        along_y(2 * pair)
-        send_along_y(2 * pair, 0)
-        along_y(2 * pair + 1)
-        send_along_y(2 * pair, 1)
-        send_along_y(2 * pair + 1, 0)
-        send_along_y(2 * pair + 1, 1)
-
-    first_stage(0)
+    c_own[...] = jnp.full(c_own.shape, count_ref[0].astype(F32), F32)
+    along_y(0)
+    group_is_here()
+    to_mate().start()
+    send_along_y(0, 0)
+    along_y(1)
+    for h, side in ((0, 1), (1, 0), (1, 1)):
+        send_along_y(h, side)
+    all_are_here()
     to_mate().wait_recv()
     c_pair[...] = c_own[...] + c_mate[...]
     for o in range(1, Z):
         pair_to(o).start()
-    first_stage(1)
+    for side in range(2):
+        along_y(2 + side)
+    for h in (2, 3):
+        for side in range(2):
+            send_along_y(h, side)
 
     base = jnp.zeros_like(c_own)
     row = c_pair[...]
@@ -355,7 +382,7 @@
                 rows = pl.ds(pl.multiple_of(k * B + half * B2, B2), B2)
                 state = x + own[h, rows, :]
                 state = cosines[h, rows, :] * state - sines[h, rows, :] * swap(state)
-                q[rows, :LANES], q[rows, LANES:] = halves(state)
+                q[rows, :LANES], q[rows, LANES:] = halves(state * (1.0 / (N * N)))
 
         repeat(Z, band)
 
@@ -390,8 +417,7 @@
         for j in range(2):
             for x_from, c_from in x_peers():
                 b_arrival(2 * pair + j, x_from, c_from).wait_recv()
-        for par in range(2):
-            for j in range(2):
+            for par in range(2):
                 def split_rows(at, par=par, j=j):
                     tiles = [weave(yb[2 * pair + j, par * XH + k, 0, pl.ds(at, 64), :],
                                    yb[2 * pair + j, par * XH + k, 1, pl.ds(at, 64), :]) for k in range(XH)]
@@ -407,21 +433,17 @@
                 parts = [dot3(lh[par, comp], ll[par, comp], xh[par, pair, k], xl[par, pair, k]) for par in range(2)]
                 if last:
                     even, odd = (eo[comp, k, par] + parts[par] for par in range(2))
-                    ob[comp, :, k * W:(k + 1) * W] = even + odd
-                    ob[comp, :, H + k * W:H + (k + 1) * W] = even - odd
+                    result[comp, :, k * W:(k + 1) * W] = even + odd
+                    result[comp, :, H + k * W:H + (k + 1) * W] = even - odd
                 else:
                     for par in range(2):
                         eo[comp, k, par] = parts[par]
-            if last:
-                pltpu.make_async_copy(ob.at[comp], result.at[comp], out_sem.at[comp]).start()
 
         repeat(2, component)
 
     back_y(0, False)
     back_y(1, True)
 
-    for comp in range(2):
-        pltpu.make_async_copy(ob.at[comp], result.at[comp], out_sem.at[comp]).wait()
     to_mate().wait_send()
     for o in range(1, Z):
         pair_to(o).wait_send()
@@ -445,13 +467,12 @@
     Y, Z, X, N = sizes
     m, H, W, B = N // X, N // 2, N // 4, N // Z
     vmem, dma = pltpu.VMEM, pltpu.SemaphoreType.DMA
-    anywhere = pl.BlockSpec(memory_space=pl.ANY)
     tile = vmem((8, LANES), F32)
     return pl.pallas_call(
         functools.partial(kernel, sizes),
         out_shape=jax.ShapeDtypeStruct((2, m, N), F32),
-        in_specs=[pl.BlockSpec(memory_space=pltpu.SMEM), anywhere, anywhere, anywhere],
-        out_specs=anywhere,
+        in_specs=[pl.BlockSpec(memory_space=pltpu.SMEM)] + [pl.BlockSpec(memory_space=pltpu.HBM)] * 3,
+        out_specs=pl.BlockSpec(memory_space=pltpu.VMEM),
         scratch_shapes=[
             vmem((2, m, N), F32),
             vmem((2, 2, H, W), BF16), vmem((2, 2, H, W), BF16),
@@ -470,7 +491,6 @@
             vmem((CHUNKS, X, 2, m // 2, LANES), F32), vmem((CHUNKS, X, 2, m // 2, LANES), F32),
             vmem((2, 2, m, W), BF16), vmem((2, 2, m, W), BF16),
             vmem((2, 2, 2, m, W), F32),
-            vmem((2, m, N), F32),
             tile, tile, tile, vmem((Z, 8, LANES), F32), tile, vmem((Y, 8, LANES), F32),
             dma((3,)),
             dma((CHUNKS, X, 2)), dma((CHUNKS, X, 2)),
@@ -479,13 +499,13 @@
             dma((CHUNKS, Z)), dma((CHUNKS, Z)),
             dma((CHUNKS, X, 2)), dma((CHUNKS, X, 2)),
             dma, dma, dma((Z,)), dma((Z,)), dma((Y,)), dma((Y,)),
-            dma((2,)),
+            pltpu.SemaphoreType.REGULAR, pltpu.SemaphoreType.REGULAR,
         ],
         compiler_params=pltpu.CompilerParams(
-            collective_id=0, has_side_effects=True, vmem_limit_bytes=60 * 1024 * 1024
+            collective_id=0, has_side_effects=True, vmem_limit_bytes=44 * 1024 * 1024
         ),
         name="wave",
-    )(counts, residual, high, low)
+    )(counts, *(pltpu.with_memory_space_constraint(a, pltpu.HBM) for a in (residual, high, low)))
 
 
 def built(split, length):
@@ -493,7 +513,7 @@
     high, low = cas_tables(length)
 
     def on_device(residual, counts):
-        return call(sizes, residual[0], counts, jnp.asarray(high), jnp.asarray(low))[None] * (1.0 / (length * length))
+        return call(sizes, residual[0], counts, jnp.asarray(high), jnp.asarray(low))[None]
 
     times = ("y", "z", "c")
     return jax.shard_map(

time: 90.8 us -> 88.8 us (0.978)
  other arithmetic: 3.22 us -> 0 us
  local copies, waits for them, and re-layouts: 0 us -> 1.32 us
    mul x1 -> x0, other arithmetic: 3.22 us -> none  [on_device(): call(sizes, residual[0], counts, jnp.asarray(high), jnp.asarray(low))[None]]
    unnamed x0 -> x1, local copies, waits for them, and re-layouts: none -> 1.32 us
where the time goes in v2:
time: 88.8 us
  Pallas kernels  86.8 us (98%)
  local copies, waits for them, and re-layouts  1.32 us (1%)
    pallas_call x1, Pallas kernels, call(): pl.pallas_call(functools.partial(kernel, sizes), out_shape=jax.ShapeDtype...  86.8 us

profile of v2, /device:TPU:1, one launch (start us, length us, event | category | flops | bytes accessed | tf_op | source)
XLA Modules:
  0.0 88.8 jit_solution(12822084960598537765)
XLA Ops:
  0.7 86.8 %wave.1 = f32[2,256,1024]{2,1,0:T(8,128)S(1)} custom-call(s32[1]{0:T(128)S(6)} %copy.6.count_ref, f32[2,256,1024]{2,1,0:T(8,128)} %bitcast.3, bf16[2,2,512,256]{3,2,1,0:T(8,128)(2,1)} %constant.4.clone.table_high, bf16[2,2,512,256]{3,2,1,0:T(8,128)(2,1)} %constant.5.clone.table_low), custom_call_target="tpu_custom_call" | custom-call | tf_op jit(solution)/shard_map/wave/pallas_call | solution.py:471
  87.4 1.3 %copy.7 = f32[1,2,256,1024]{3,2,1,0:T(8,128)} copy(f32[1,2,256,1024]{3,2,1,0:T(8,128)S(1)} %bitcast.2) | data formatting | bytes 4194304

commit v3 on v2

--- a/solution.py
+++ b/solution.py
@@ -159,15 +159,16 @@
     def row_to(o):
         return remote(c_row, c_y.at[o], cy_send.at[o], cy_recv.at[o], y=lax.rem(yi + o, Y))
 
+    def fold_rows(par):
+        sign = jnp.where(par == 0, 1.0, -1.0)
+        for comp in range(2):
+            def split_rows(at, comp=comp):
+                rows = pl.ds(at, 32)
+                sdh[par, comp, rows, :], sdl[par, comp, rows, :] = halves(r[comp, rows, :H] + sign * r[comp, rows, H:])
+            chunks(m, 32, split_rows)
+
     loads[0].wait()
-    for comp in range(2):
-        def split_rows(at, comp=comp):
-            rows = pl.ds(at, 32)
-            first, second = r[comp, rows, :H], r[comp, rows, H:]
-            sdh[0, comp, rows, :], sdl[0, comp, rows, :] = halves(first + second)
-            sdh[1, comp, rows, :], sdl[1, comp, rows, :] = halves(first - second)
-        chunks(m, 32, split_rows)
-
+    fold_rows(1 - xi // XH)
     loads[1].wait()
     loads[2].wait()
 
@@ -209,6 +210,7 @@
     group_is_here()
     to_mate().start()
     send_along_y(0, 0)
+    fold_rows(xi // XH)
     along_y(1)
     for h, side in ((0, 1), (1, 0), (1, 1)):
         send_along_y(h, side)
@@ -292,7 +294,7 @@
             chunks(m2, 64, split_rows)
 
         def quarter(i):
-            g = lax.rem(zi // nb + 2 + i, 4)
+            g = lax.rem(zi // nb + jnp.where(i < 2, 2 - i, 9 - 3 * i), 4)
             par, half = g // 2, lax.rem(g, 2)
             high = jnp.concatenate([xh[par, half, 0], xh[par, half, 1]], axis=1)
             low = jnp.concatenate([xl[par, half, 0], xl[par, half, 1]], axis=1)
@@ -358,12 +360,13 @@
     totals(0)
     forward(3)
 
+    prefix(0)
+
     def middle(i):
         totals(i + 1)
-        prefix(i)
+        prefix(i + 1)
 
     repeat(3, middle)
-    prefix(3)
 
     def b_copy(h, x_to, t):
         return remote(xs.at[h, x_to, t], yb.at[h, xi, ci], b_send.at[h, x_to, t], b_recv.at[h, xi, ci], x=x_to, c=t)
@@ -373,9 +376,6 @@
                       b_recv.at[h, x_from, c_from], x=x_from, c=c_from)
 
     def back_x(h):
-        for z_from in z_peers():
-            p_arrival(h, z_from).wait_recv()
-
         def band(k):
             before = pb[h, k]
             for half, x in enumerate(cross(before, before)):
@@ -384,10 +384,13 @@
                 state = cosines[h, rows, :] * state - sines[h, rows, :] * swap(state)
                 q[rows, :LANES], q[rows, LANES:] = halves(state * (1.0 / (N * N)))
 
-        repeat(Z, band)
+        band(zi)
+        for z_from in z_peers():
+            p_arrival(h, z_from).wait_recv()
+            band(z_from)
 
         def block(i):
-            k = lax.rem(xi + 1 + i, XH)
+            k = lax.rem(xi + i, XH)
             rows = pl.ds(pl.multiple_of(k * m, m), m)
             parts = []
             for par in range(2):

time: 88.8 us -> 87.2 us (0.982)
  Pallas kernels: 86.8 us -> 85.1 us
    pallas_call x1, Pallas kernels: 86.8 us -> 85.1 us  [call(): pl.pallas_call(functools.partial(kernel, sizes), out_shape=jax.ShapeDtype...]
where the time goes in v3:
time: 87.2 us; the launch traced here: 87.1 us
  Pallas kernels  85.1 us (98%)
  local copies, waits for them, and re-layouts  1.32 us (2%)
    pallas_call x1, Pallas kernels, call(): pl.pallas_call(functools.partial(kernel, sizes), out_shape=jax.ShapeDtype...  85.1 us

profile of v3, /device:TPU:1, one launch (start us, length us, event | category | flops | bytes accessed | tf_op | source)
XLA Modules:
  0.0 87.1 jit_solution(371538050909822415)
XLA Ops:
  0.7 85.1 %wave.1 = f32[2,256,1024]{2,1,0:T(8,128)S(1)} custom-call(s32[1]{0:T(128)S(6)} %copy.6.count_ref, f32[2,256,1024]{2,1,0:T(8,128)} %bitcast.3, bf16[2,2,512,256]{3,2,1,0:T(8,128)(2,1)} %constant.4.clone.table_high, bf16[2,2,512,256]{3,2,1,0:T(8,128)(2,1)} %constant.5.clone.table_low), custom_call_target="tpu_custom_call" | custom-call | tf_op jit(solution)/shard_map/wave/pallas_call | solution.py:474
  85.8 1.3 %copy.7 = f32[1,2,256,1024]{3,2,1,0:T(8,128)} copy(f32[1,2,256,1024]{3,2,1,0:T(8,128)S(1)} %bitcast.2) | data formatting | bytes 4194304

commit v4 on v3

--- a/solution.py
+++ b/solution.py
@@ -248,15 +248,16 @@
     rates = jnp.where(first_half, (base + first_count)[:1], (base + c_pair[...])[:1]) * (phase_rate / math.pi)
     terms = [jnp.where(w_lanes, s, c) for s, c in zip(SIN_TERMS, COS_TERMS)]
     column = lax.rem(lane, FOLD)
+    rows_apart = (2 * lax.broadcasted_iota(jnp.int32, (64, LANES), 0)).astype(F32)
 
     def angles(h):
         col = h * LANES + lax.rem(xi, XH) * 2 * FOLD + ci * FOLD + column
         wave_y = signed(2 * col + xi // XH, N)
+        wave_y_squared = wave_y * wave_y
 
         def rows_of(at):
-            place = at + lax.broadcasted_iota(jnp.int32, (64, LANES), 0)
-            wave_x = signed(2 * lax.rem(place, H) + place // H, N)
-            turns = jnp.sqrt(wave_x * wave_x + wave_y * wave_y) * rates
+            wave_x = rows_apart + signed(2 * lax.rem(at, H) + at // H, N)
+            turns = jnp.sqrt(wave_x * wave_x + wave_y_squared) * rates
             nearest = jnp.floor(turns + 0.5)
             f = turns - nearest
             g = f * f

time: 87.2 us -> 86.7 us (level)
  no operation moved by 1% of the time
where the time goes in v4:
time: 86.7 us; the launch traced here: 86.6 us
  Pallas kernels  84.7 us (98%)
  local copies, waits for them, and re-layouts  1.32 us (2%)
    pallas_call x1, Pallas kernels, call(): pl.pallas_call(functools.partial(kernel, sizes), out_shape=jax.ShapeDtype...  84.7 us

profile of v4, /device:TPU:1, one launch (start us, length us, event | category | flops | bytes accessed | tf_op | source)
XLA Modules:
  0.0 86.6 jit_solution(5761440187192799364)
XLA Ops:
  0.7 84.7 %wave.1 = f32[2,256,1024]{2,1,0:T(8,128)S(1)} custom-call(s32[1]{0:T(128)S(6)} %copy.6.count_ref, f32[2,256,1024]{2,1,0:T(8,128)} %bitcast.3, bf16[2,2,512,256]{3,2,1,0:T(8,128)(2,1)} %constant.4.clone.table_high, bf16[2,2,512,256]{3,2,1,0:T(8,128)(2,1)} %constant.5.clone.table_low), custom_call_target="tpu_custom_call" | custom-call | tf_op jit(solution)/shard_map/wave/pallas_call | solution.py:475
  85.3 1.3 %copy.7 = f32[1,2,256,1024]{3,2,1,0:T(8,128)} copy(f32[1,2,256,1024]{3,2,1,0:T(8,128)S(1)} %bitcast.2) | data formatting | bytes 4194304

commit v5 on v4

--- a/solution.py
+++ b/solution.py
@@ -431,19 +431,32 @@
                             rows = pl.ds(pl.multiple_of(half * m2 + at, 64), 64)
                             lh[par, comp, rows, lanes], ll[par, comp, rows, lanes] = halves(x)
                 chunks(m2, 64, split_rows)
+            if last:
+                def accumulate(comp, j=j):
+                    waves = slice(j * LANES, (j + 1) * LANES)
+                    for k in range(2):
+                        parts = []
+                        for par in range(2):
+                            high, low = lh[par, comp, :, waves], ll[par, comp, :, waves]
+                            table = xh[par, pair, k, waves, :]
+                            both = jnp.dot(jnp.concatenate([high, low], axis=1), jnp.concatenate([table, table], axis=0),
+                                           preferred_element_type=F32)
+                            rest = jnp.dot(high, xl[par, pair, k, waves, :], preferred_element_type=F32)
+                            parts.append(eo[comp, k, par] + (both + rest))
+                        if j == 0:
+                            eo[comp, k, 0], eo[comp, k, 1] = parts
+                        else:
+                            result[comp, :, k * W:(k + 1) * W] = parts[0] + parts[1]
+                            result[comp, :, H + k * W:H + (k + 1) * W] = parts[0] - parts[1]
+                repeat(2, accumulate)
 
         def component(comp):
             for k in range(2):
-                parts = [dot3(lh[par, comp], ll[par, comp], xh[par, pair, k], xl[par, pair, k]) for par in range(2)]
-                if last:
-                    even, odd = (eo[comp, k, par] + parts[par] for par in range(2))
-                    result[comp, :, k * W:(k + 1) * W] = even + odd
-                    result[comp, :, H + k * W:H + (k + 1) * W] = even - odd
-                else:
-                    for par in range(2):
-                        eo[comp, k, par] = parts[par]
-
-        repeat(2, component)
+                for par in range(2):
+                    eo[comp, k, par] = dot3(lh[par, comp], ll[par, comp], xh[par, pair, k], xl[par, pair, k])
+
+        if not last:
+            repeat(2, component)
 
     back_y(0, False)
     back_y(1, True)

time: 86.7 us -> 86.4 us (level)
  no operation moved by 1% of the time
where the time goes in v5:
time: 86.4 us; the launch traced here: 86.3 us
  Pallas kernels  84.4 us (98%)
  local copies, waits for them, and re-layouts  1.32 us (2%)
    pallas_call x1, Pallas kernels, call(): pl.pallas_call(functools.partial(kernel, sizes), out_shape=jax.ShapeDtype...  84.4 us

profile of v5, /device:TPU:1, one launch (start us, length us, event | category | flops | bytes accessed | tf_op | source)
XLA Modules:
  0.0 86.3 jit_solution(8218459481428075637)
XLA Ops:
  0.7 84.4 %wave.1 = f32[2,256,1024]{2,1,0:T(8,128)S(1)} custom-call(s32[1]{0:T(128)S(6)} %copy.6.count_ref, f32[2,256,1024]{2,1,0:T(8,128)} %bitcast.3, bf16[2,2,512,256]{3,2,1,0:T(8,128)(2,1)} %constant.4.clone.table_high, bf16[2,2,512,256]{3,2,1,0:T(8,128)(2,1)} %constant.5.clone.table_low), custom_call_target="tpu_custom_call" | custom-call | tf_op jit(solution)/shard_map/wave/pallas_call | solution.py:488
  85.0 1.3 %copy.7 = f32[1,2,256,1024]{3,2,1,0:T(8,128)} copy(f32[1,2,256,1024]{3,2,1,0:T(8,128)S(1)} %bitcast.2) | data formatting | bytes 4194304
